TPU v7x, 32 devices: a whole 2x2x4 slice. The times are simulated.
32 devices in a mesh: row: 4 (over y, core), col: 8 (over z, x).
Axes of the slice: x: 2, y: 2, z: 4, core: 2. Of those that a mesh axis runs over, the one named last changes fastest.
Arguments:
- templates: float32 [96, 3, 1024], P(('row', 'col')), may hold values from -600 to 600
Outputs:
- similar: float32 [96, 96], P(('row', 'col'))
All inputs are finite; a program needn't handle non-finite values.
Results may differ from a plain program's by a relative error of at most 0.0012.
Values may be sent and summed in bfloat16 or wider, within the bound.
A program may use at most 128 MiB of HBM per device.

v0:
```python
import math

import jax
import jax.numpy as jnp
from jax import lax
from jax.sharding import PartitionSpec as P

LAGS = 512


def normalize(templates):
    scaling = lax.rsqrt(jnp.mean(templates * templates, axis=2, keepdims=True) + 1e-06) / math.sqrt(
        templates.shape[2]
    )
    return (templates * scaling).astype(jnp.bfloat16)


def forward_table(samples, transform_len):
    half_len = transform_len // 2
    sample_idx = jnp.arange(samples, dtype=jnp.int32)[:, None]
    slot_idx = jnp.arange(transform_len, dtype=jnp.int32)[None, :]
    freq_idx = jnp.where(slot_idx < half_len, slot_idx, slot_idx - half_len)
    phases = sample_idx * freq_idx % transform_len
    angles = phases.astype(jnp.float32) * (2.0 * math.pi / transform_len)
    nyquist = jnp.where(sample_idx % 2 == 0, 1.0, -1.0)
    basis = jnp.where(
        slot_idx < half_len,
        jnp.cos(angles),
        jnp.where(slot_idx == half_len, nyquist, -jnp.sin(angles)),
    )
    return basis.astype(jnp.bfloat16)


def inverse_table(transform_len, lag_total):
    half_len = transform_len // 2
    slot_idx = jnp.arange(transform_len, dtype=jnp.int32)[:, None]
    lag_idx = jnp.arange(lag_total, dtype=jnp.int32)[None, :] - lag_total // 2
    freq_idx = jnp.where(slot_idx < half_len, slot_idx, slot_idx - half_len)
    phases = freq_idx * lag_idx % transform_len
    angles = phases.astype(jnp.float32) * (2.0 * math.pi / transform_len)
    weight = jnp.where(freq_idx == 0, 1.0, 2.0) / transform_len
    nyquist = jnp.where(lag_idx % 2 == 0, 1.0, -1.0) / transform_len
    basis = jnp.where(
        slot_idx < half_len,
        weight * jnp.cos(angles),
        jnp.where(slot_idx == half_len, nyquist, -weight * jnp.sin(angles)),
    )
    return basis.astype(jnp.bfloat16)


def spectra_of(normed, basis):
    row_total, comps, samples = normed.shape
    flattened = normed.reshape(row_total * comps, samples)
    spectrum = jnp.dot(flattened, basis, preferred_element_type=jnp.float32)
    return spectrum.astype(jnp.bfloat16).reshape(row_total, comps, basis.shape[1])


def pair_einsum(left_part, right_part):
    return jnp.einsum("icf,jcf->ijf", left_part.astype(jnp.float32), right_part.astype(jnp.float32))


def similarity(left_spec, right_spec, inverse):
    half_len = left_spec.shape[2] // 2
    left_real = left_spec[:, :, :half_len]
    left_imag = left_spec[:, :, half_len:]
    right_real = right_spec[:, :, :half_len]
    right_imag = right_spec[:, :, half_len:]
    above_zero = jnp.arange(half_len, dtype=jnp.int32) >= 1
    right_masked = jnp.where(above_zero, right_imag, jnp.zeros_like(right_imag))
    left_masked = jnp.where(above_zero, left_real, jnp.zeros_like(left_real))
    right_turned = jnp.where(above_zero, -right_real, right_imag)
    even_part = pair_einsum(
        jnp.concatenate([left_real, left_imag], axis=1),
        jnp.concatenate([right_real, right_masked], axis=1),
    )
    odd_part = pair_einsum(
        jnp.concatenate([left_masked, left_imag], axis=1),
        jnp.concatenate([right_imag, right_turned], axis=1),
    )
    cross_spec = jnp.concatenate([even_part, odd_part], axis=2).astype(jnp.bfloat16)
    left_rows = left_spec.shape[0]
    right_rows = right_spec.shape[0]
    lagged = jnp.dot(
        cross_spec.reshape(left_rows * right_rows, 2 * half_len),
        inverse,
        preferred_element_type=jnp.float32,
    )
    return jnp.max(lagged, axis=1).reshape(left_rows, right_rows)


def body(templates):
    per_device = templates.shape[0]
    samples = templates.shape[2]
    transform_len = samples + LAGS // 2
    forward = forward_table(samples, transform_len)
    inverse = inverse_table(transform_len, LAGS)
    local_waves = normalize(templates)

    def finish(received):
        return spectra_of(received, forward)

    row_count = lax.axis_size("row")
    col_count = lax.axis_size("col")
    partners = finish(lax.all_gather(local_waves, "row", axis=0, tiled=True))
    pair_block = similarity(
        finish(lax.all_gather(local_waves, "col", axis=0, tiled=True)), partners, inverse
    )
    owned_rows = lax.all_to_all(pair_block, "col", split_axis=0, concat_axis=1, tiled=True)
    reordered = owned_rows.reshape(per_device, col_count, row_count, per_device).transpose(
        0, 2, 1, 3
    )
    return reordered.reshape(per_device, col_count * row_count * per_device)


def solution(mesh):
    placed = (P(("row", "col"), None, None),)
    return jax.shard_map(
        body, mesh=mesh, in_specs=placed, out_specs=P(("row", "col"), None), check_vma=False
    )
```

profile of v0, /device:TPU:0, one launch (start us, length us, event | category | flops | bytes accessed | tf_op | source)
XLA Modules:
  0.0 132.2 jit_solution(18029186734584677094)
XLA Ops:
  0.0 0.9 multiply_reduce_fusion
  0.9 0.9 multiply_convert_fusion
  1.8 6.4 %all_gather.6 = bf16[12,3,1024]{2,1,0:T(4,128)(2,1)S(1)} all-gather(bf16[3,3,1024]{2,1,0:T(4,128)(2,1)S(1)} %multiply_convert_fusion), channel_id=1, replica_groups=mesh['row'=4,'col'=8] {'row'}, dimensions={0}, use_global_device_ids=true | all-gather | bytes 92160 | tf_op jit(solution)/shard_map/all_gather | solution.py:104
  8.2 31.4 %all_gather.7 = bf16[24,3,1024]{2,1,0:T(4,128)(2,1)S(1)} all-gather(bf16[3,3,1024]{2,1,0:T(4,128)(2,1)S(1)} %multiply_convert_fusion), channel_id=1, replica_groups=mesh['row'=4,'col'=8] {'col'}, dimensions={0}, use_global_device_ids=true | all-gather | bytes 165888 | tf_op jit(solution)/shard_map/all_gather | solution.py:106
  39.7 22.6 %fusion.13 = bf16[36,1280]{1,0:T(8,128)(2,1)S(1)} fusion(bf16[36,1024]{1,0:T(8,128)(2,1)S(1)} %reshape.135, bf16[1024]{0:T(1024)(128)(2,1)S(1)} %fusion.35, s32[1280]{0:T(1024)S(1)} %add_select_fusion.2, pred[1280]{0:T(1024)(128)(4,1)S(1)} %get-tuple-element.11, pred[1280]{0:T(1024)(128)(4,1)S(1)} %get-tuple-element.12), kind=kOutput, calls=%fused_computation.21 | convolution fusion | flops 110146560 | bytes 175616 | tf_op jit(solution)/shard_map/dot_general | solution.py:54
  62.6 1.9 %copy.30 = bf16[12,6,640]{0,1,2:T(8,128)(2,1)} copy(bf16[12,6,640]{2,1,0:T(8,128)(2,1)S(1)} %pad_maximum_fusion.5) | data formatting | bytes 184320 | tf_op jit(solution)/shard_map/concatenate | solution.py:78
  64.5 0.1 reshape.137
  64.7 22.9 %fusion.12 = bf16[72,1280]{1,0:T(8,128)(2,1)S(1)} fusion(bf16[72,1024]{1,0:T(8,128)(2,1)S(1)} %reshape.137, bf16[1024]{0:T(1024)(128)(2,1)S(1)} %fusion.35, s32[1280]{0:T(1024)S(1)} %add_select_fusion.2, pred[1280]{0:T(1024)(128)(4,1)S(1)} %get-tuple-element.11, pred[1280]{0:T(1024)(128)(4,1)S(1)} %get-tuple-element.12), kind=kOutput, calls=%fused_computation.20 | convolution fusion | flops 204564480 | bytes 341504 | tf_op jit(solution)/shard_map/dot_general | solution.py:54
  87.6 0.1 reshape.138
  87.8 0.4 copy.34
  88.2 3.1 %broadcast_select_fusion = bf16[24,3,640]{0,1,2:T(4,128)(2,1)} fusion(bf16[24,3,640]{0,1,2:T(4,128)(2,1)S(1)} %copy.34, pred[640]{0:T(1024)(128)(4,1)S(1)} %iota_compare_fusion.2), kind=kLoop, calls=%fused_computation.41 | loop fusion | flops 46080 | bytes 184960 | tf_op jit(solution)/shard_map/jit(_where)/select_n | solution.py:70
  91.3 0.4 copy.35
  91.7 3.0 %convert_bitcast_fusion = bf16[24,12,640]{0,1,2:T(8,128)(2,1)S(1)} fusion(bf16[12,6,640]{0,1,2:T(8,128)(2,1)} %copy.30, bf16[24,3,640]{0,1,2:T(4,128)(2,1)S(1)} %copy.35, bf16[24,3,640]{0,1,2:T(4,128)(2,1)} %broadcast_select_fusion), kind=kOutput, calls=%fused_computation.15 | convolution fusion | flops 2764800 | bytes 645120 | tf_op jit(solution)/shard_map/icf,jcf->ijf/dot_general | solution.py:59
  94.7 2.7 %copy.31 = bf16[24,12,640]{2,1,0:T(8,128)(2,1)} copy(bf16[24,12,640]{0,1,2:T(8,128)(2,1)S(1)} %convert_bitcast_fusion) | data formatting | bytes 737280 | tf_op jit(solution)/shard_map/icf,jcf->ijf/transpose | solution.py:59
  97.4 1.9 %concatenate.26 = bf16[288,640]{1,0:T(8,128)(2,1)} reshape(bf16[24,12,640]{2,1,0:T(8,128)(2,1)} %copy.31) | data formatting | bytes 737280 | tf_op jit(solution)/shard_map/concatenate | solution.py:80
  99.3 1.9 %copy.28 = bf16[12,6,640]{0,1,2:T(8,128)(2,1)} copy(bf16[12,6,640]{2,1,0:T(8,128)(2,1)S(1)} %pad_maximum_fusion.4) | data formatting | bytes 184320 | tf_op jit(solution)/shard_map/concatenate | solution.py:74
  101.3 3.0 %convert_bitcast_fusion.1 = bf16[24,12,640]{0,1,2:T(8,128)(2,1)S(1)} fusion(bf16[12,6,640]{0,1,2:T(8,128)(2,1)} %copy.28, bf16[24,3,640]{0,1,2:T(4,128)(2,1)S(1)} %copy.35, bf16[24,3,640]{0,1,2:T(4,128)(2,1)} %copy-done), kind=kOutput, calls=%fused_computation.16 | convolution fusion | flops 2764800 | bytes 645120 | tf_op jit(solution)/shard_map/icf,jcf->ijf/dot_general | solution.py:59
  104.2 2.3 %copy.29 = bf16[24,12,640]{2,1,0:T(8,128)(2,1)S(1)} copy(bf16[24,12,640]{0,1,2:T(8,128)(2,1)S(1)} %convert_bitcast_fusion.1) | data formatting | bytes 737280 | tf_op jit(solution)/shard_map/icf,jcf->ijf/transpose | solution.py:59
  106.6 12.7 %fusion.27 = f32[288]{0:T(512)S(1)} fusion(f32[1280]{0:T(1024)S(1)} %get-tuple-element.14, bf16[512]{0:T(512)(128)(2,1)S(1)} %select_multiply_fusion.1, s32[512]{0:T(512)S(1)} %iota_add_fusion, s32[1280]{0:T(1024)S(1)} %add_select_fusion.2, f32[1280]{0:T(1024)S(1)} %get-tuple-element.13, pred[1280]{0:T(1024)(128)(4,1)S(1)} %get-tuple-element.11, ...), kind=kOutput, calls=%fused_computation.37 | convolution fusion | flops 387628768 | bytes 759424 | tf_op jit(solution)/shard_map/dot_general | solution.py:83
  119.4 0.1 all_to_all.12
  119.5 11.8 %all_to_all.16 = f32[8,3,12]{2,1,0:T(4,128)S(1)} all-to-all(f32[8,3,12]{2,1,0:T(4,128)S(1)} %all_to_all.12), channel_id=1, replica_groups=mesh['row'=4,'col'=8] {'col'}, dimensions={0} | all-to-all | bytes 2304 | tf_op jit(solution)/shard_map/all_to_all | solution.py:108
  131.3 0.1 copy.32
  131.4 0.1 copy.33
  131.5 0.7 reshape.140
  (17 shorter events, 0.6 us)
Async XLA Ops:
  88.2 3.1 %copy-start = (bf16[24,3,640]{0,1,2:T(4,128)(2,1)}, bf16[24,3,640]{0,1,2:T(4,128)(2,1)S(1)}, u32[]{:S(2)}) copy-start(bf16[24,3,640]{0,1,2:T(4,128)(2,1)S(1)} %copy.34) | copy-start | bytes 276484
where the time goes:
time: 133 us; the launch traced here: 132 us
  matrix products  64.2 us (48%)
  blocking collectives  49.6 us (37%)
  local copies, waits for them, and re-layouts  13.1 us (10%)
  other arithmetic  5.17 us (4%)
    dot_general x2, matrix products, spectra_of(): spectrum = jnp.dot(flattened, basis, preferred_element_type=jnp.float32)  45.5 us
    all_gather x1, blocking collectives, body(): lax.all_gather(local_waves, 'col', axis=0, tiled=True)  31.4 us
    dot_general x1, matrix products, similarity(): jnp.dot(cross_spec.reshape(left_rows * right_rows, 2 * half_len), inverse...  12.7 us
    all_to_all x1, blocking collectives, body(): lax.all_to_all(pair_block, 'col', split_axis=0, concat_axis=1, tiled=True)  11.8 us
    all_gather x1, blocking collectives, body(): partners = finish(lax.all_gather(local_waves, 'row', axis=0, tiled=True))  6.37 us
    dot_general x2, matrix products, pair_einsum(): jnp.einsum('icf,jcf->ijf', left_part.astype(jnp.float32), right_part.asty...  5.94 us
    transpose x2, local copies, waits for them, and re-layouts, pair_einsum(): jnp.einsum('icf,jcf->ijf', left_part.astype(jnp.float32), right_part.asty...  5.02 us
    select_n x1, other arithmetic, similarity(): left_masked = jnp.where(above_zero, left_real, jnp.zeros_like(left_real))  3.12 us

commit v1 on v0

v1 whole, which is shorter than its diff:
```python
import functools
import math

import jax
import jax.numpy as jnp
from jax import lax
from jax.experimental import pallas as pl
from jax.experimental.pallas import tpu as pltpu
from jax.sharding import PartitionSpec as P

LAGS = 512
LANES = 128
SUBS = 8
CORES = 2
MESH = pl.DeviceIdType.MESH


def each(count, step):
    if count <= 8:
        for k in range(count):
            step(k)
    else:
        lax.fori_loop(0, count, lambda k, carry: (step(k), carry)[1], 0)


def kernel(
    rows, cols, x_ref, out_ref, stage, gathered, toeplitz, flat, waves, send_sem, recv_sem
):
    n, comps, samples = x_ref.shape
    chunks = samples // LANES
    span = samples + LANES
    width = samples + 2 * LANES
    devices = rows * cols
    tall = rows // CORES
    wide = 2 ** int(math.log2(math.sqrt(cols)))
    deep = cols // wide
    plane = tall * wide
    row = lax.axis_index("row")
    col = lax.axis_index("col")
    my_y, my_core = row // CORES, row % CORES
    my_z, my_x = col // wide, col % wide
    my_xy = my_y * wide + my_x

    def place(xy, z, core):
        return (xy // wide) * CORES + core, z * wide + xy % wide

    def slot_of(xy, z, core):
        r, c = place(xy, z, core)
        return r * cols + c

    def up(k):
        return (my_z + 1 + k) % deep

    def beside(k):
        return (my_xy + 1 + k) % plane

    other = 1 - my_core
    mine = slot_of(my_xy, my_z, my_core)

    barrier = pltpu.get_barrier_semaphore()

    def greet(xy, z, core):
        pl.semaphore_signal(
            barrier, inc=1, device_id=place(xy, z, core), device_id_type=MESH
        )

    each(deep - 1, lambda k: greet(my_xy, up(k), my_core))
    each(plane - 1, lambda k: greet(beside(k), my_z, my_core))
    greet(my_xy, my_z, other)

    normed = []
    for t in range(n):
        x = x_ref[t]
        scale = lax.rsqrt(jnp.mean(x * x, axis=1, keepdims=True) + 1e-06) / math.sqrt(samples)
        rounded = (x * scale).astype(jnp.bfloat16).astype(jnp.float32)
        normed.append(rounded)
        for q in range(chunks):
            stage[pl.ds(t * comps * chunks + q, comps, stride=chunks), :] = rounded[
                :, q * LANES : (q + 1) * LANES
            ]
    gathered[mine] = stage[...].reshape(n * comps, chunks, LANES).astype(jnp.bfloat16)
    pl.semaphore_wait(barrier, deep - 1 + plane - 1 + 1)

    def copy(slot, to, sem):
        return pltpu.make_async_remote_copy(
            src_ref=gathered.at[slot],
            dst_ref=gathered.at[slot],
            send_sem=send_sem.at[sem],
            recv_sem=recv_sem.at[slot],
            device_id=to,
            device_id_type=MESH,
        )

    def to_sibling(slot):
        return copy(slot, place(my_xy, my_z, other), slot)

    def to_plane(slot, z, k):
        return copy(slot, place(beside(k), my_z, my_core), devices + z * plane + k)

    def to_column(k):
        return copy(mine, place(my_xy, up(k), my_core), devices + deep * plane + k)

    def arrived(slot):
        to_sibling(slot).wait_recv()

    each(deep - 1, lambda k: to_column(k).start())
    each(plane - 1, lambda k: to_plane(mine, my_z, k).start())
    to_sibling(mine).start()

    def build(t, c):
        line = jnp.concatenate(
            [normed[t][c : c + 1], jnp.zeros((1, LANES), jnp.float32)], axis=1
        )
        shifted = pltpu.roll(
            jnp.broadcast_to(line, (LANES, span)), 0, axis=1, stride=1, stride_axis=0
        )
        toeplitz[t * LANES : (t + 1) * LANES, c * span : (c + 1) * span] = shifted.astype(
            jnp.bfloat16
        )

    for t in range(1):
        for c in range(comps):
            build(t, c)

    def pass_on(k):
        z = up(k)
        slot = slot_of(my_xy, z, my_core)
        arrived(slot)
        each(plane - 1, lambda m: to_plane(slot, z, m).start())
        to_sibling(slot).start()

    each(deep - 1, pass_on)

    for t in range(1, n):
        for c in range(comps):
            build(t, c)
    rows_block = waves.shape[0]
    for c in range(comps):
        for at in (0, LANES + samples):
            waves[:, c * width + at : c * width + at + LANES] = jnp.zeros(
                (rows_block, LANES), jnp.bfloat16
            )

    def hand_over(k):
        slot = slot_of(beside(k // deep), (my_z + k % deep) % deep, my_core)
        arrived(slot)
        to_sibling(slot).start()

    each_loop = (plane - 1) * deep
    lax.fori_loop(0, each_loop, lambda k, carry: (hand_over(k), carry)[1], 0)

    def from_sibling(k, carry):
        arrived(slot_of(k // deep, k % deep, other))
        return carry

    lax.fori_loop(0, plane * deep, from_sibling, 0)

    def left(k, carry):
        to_sibling(slot_of(k // deep, k % deep, my_core)).wait_send()
        return carry

    lax.fori_loop(0, plane * deep, left, 0)

    def left_plane(k, carry):
        to_plane(mine, k // (plane - 1), k % (plane - 1)).wait_send()
        return carry

    lax.fori_loop(0, deep * (plane - 1), left_plane, 0)
    each(deep - 1, lambda k: to_column(k).wait_send())

    block = rows_block // n
    stride = comps * chunks

    def compare(b):
        flat[...] = (
            gathered[pl.ds(b * block, block)]
            .astype(jnp.float32)
            .reshape(block * n * comps * chunks, LANES)
        )
        for c in range(comps):
            for q in range(chunks):
                at = c * width + (q + 1) * LANES
                waves[:, at : at + LANES] = flat[
                    pl.ds(c * chunks + q, rows_block, stride=stride), :
                ].astype(jnp.bfloat16)

        best = None
        for lag0 in range(-LAGS // 2, LAGS // 2, 2 * LANES):
            low = max(0, -lag0 - LANES)
            total = None
            for c in range(comps):
                left_part = toeplitz[:, c * span + low : c * span + low + samples]
                at = c * width + LANES + low + lag0
                right_part = jnp.concatenate(
                    [waves[:, at : at + samples], waves[:, at + LANES : at + LANES + samples]],
                    axis=0,
                )
                part = lax.dot_general(
                    left_part,
                    right_part,
                    (((1,), (1,)), ((), ())),
                    preferred_element_type=jnp.float32,
                )
                total = part if total is None else total + part
            top = jnp.max(total.reshape(n, LANES, 2 * rows_block), axis=1)
            best = top if best is None else jnp.maximum(best, top)
        out_ref[b] = jnp.maximum(best[:, :rows_block], best[:, rows_block:])

    each(devices // block, compare)


def body(templates):
    n, comps, samples = templates.shape
    rows = lax.axis_size("row")
    cols = lax.axis_size("col")
    devices = rows * cols
    block = math.gcd(devices, 32)
    chunks = samples // LANES
    span = samples + LANES
    width = samples + 2 * LANES
    vmem = pl.BlockSpec(memory_space=pltpu.VMEM)
    out = pl.pallas_call(
        functools.partial(kernel, rows, cols),
        out_shape=jax.ShapeDtypeStruct((devices // block, n, block * n), jnp.float32),
        in_specs=[vmem],
        out_specs=vmem,
        scratch_shapes=[
            pltpu.VMEM((n * comps * chunks, LANES), jnp.float32),
            pltpu.VMEM((devices, n * comps, chunks, LANES), jnp.bfloat16),
            pltpu.VMEM((n * LANES, comps * span), jnp.bfloat16),
            pltpu.VMEM((block * n * comps * chunks, LANES), jnp.float32),
            pltpu.VMEM((block * n, comps * width), jnp.bfloat16),
            pltpu.SemaphoreType.DMA((2 * devices + cols,)),
            pltpu.SemaphoreType.DMA((devices,)),
        ],
        compiler_params=pltpu.CompilerParams(collective_id=0, has_side_effects=True),
    )(templates)
    return out.transpose(1, 0, 2).reshape(n, devices * n)


def solution(mesh):
    placed = (P(("row", "col"), None, None),)
    return jax.shard_map(
        body, mesh=mesh, in_specs=placed, out_specs=P(("row", "col"), None), check_vma=False
    )
```

time: 133 us -> 19 us (0.14)
  matrix products: 64.2 us -> 0 us
  blocking collectives: 49.6 us -> 0 us
  Pallas kernels: 0 us -> 17.4 us
  local copies, waits for them, and re-layouts: 13.1 us -> 1.26 us
  other arithmetic: 5.17 us -> 0 us
    dot_general x5 -> x0, matrix products: 64.2 us -> none  [the longest x2 45.5 us: spectra_of(): spectrum = jnp.dot(flattened, basis, preferred_element_type=jnp.float32)]
    all_gather x2 -> x0, blocking collectives: 37.8 us -> none  [the longest x1 31.4 us: body(): lax.all_gather(local_waves, 'col', axis=0, tiled=True)]
    pallas_call x0 -> x1, Pallas kernels: none -> 17.4 us  [body(): pl.pallas_call(functools.partial(kernel, rows, cols), out_shape=jax.Shape...]
    all_to_all x1 -> x0, blocking collectives: 11.8 us -> none  [body(): lax.all_to_all(pair_block, 'col', split_axis=0, concat_axis=1, tiled=True)]
    concatenate x4 -> x0, local copies, waits for them, and re-layouts: 5.78 us -> none  [the longest x2 1.95 us: similarity(): jnp.concatenate([even_part, odd_part], axis=2).astype(jnp.bfloat16)]
    transpose x3 -> x0, local copies, waits for them, and re-layouts: 5.17 us -> none  [the longest x2 5.02 us: pair_einsum(): jnp.einsum('icf,jcf->ijf', left_part.astype(jnp.float32), right_part.asty...]
    select_n x4 -> x0, other arithmetic: 3.22 us -> none  [the longest x1 3.12 us: similarity(): left_masked = jnp.where(above_zero, left_real, jnp.zeros_like(left_real))]
where the time goes in v1:
time: 19 us; the launch traced here: 18.7 us
  Pallas kernels  17.4 us (92%)
  local copies, waits for them, and re-layouts  1.26 us (7%)
    pallas_call x1, Pallas kernels, body(): pl.pallas_call(functools.partial(kernel, rows, cols), out_shape=jax.Shape...  17.4 us
    unnamed x1, local copies, waits for them, and re-layouts  1.26 us

profile of v1, /device:TPU:0, one launch (start us, length us, event | category | flops | bytes accessed | tf_op | source)
XLA Modules:
  0.0 18.7 jit_solution(4226920342952354417)
XLA Ops:
  0.0 17.4 %shard_map.17 = f32[1,3,96]{2,1,0:T(4,128)} custom-call(f32[3,3,1024]{2,1,0:T(4,128)} %x_ref.1), custom_call_target="tpu_custom_call" | custom-call | tf_op jit(solution)/shard_map/pallas_call | solution.py:222
  17.4 1.3 %copy.3 = f32[3,96]{1,0:T(4,128)} copy(f32[3,96]{1,0:T(4,128)} %bitcast.1) | data formatting | bytes 2304

commit v2 on v1

--- a/solution.py
+++ b/solution.py
@@ -3,6 +3,7 @@
 
 import jax
 import jax.numpy as jnp
+import numpy as np
 from jax import lax
 from jax.experimental import pallas as pl
 from jax.experimental.pallas import tpu as pltpu
@@ -13,6 +14,39 @@
 SUBS = 8
 CORES = 2
 MESH = pl.DeviceIdType.MESH
+
+
+def forward_table(samples, transform_len):
+    half_len = transform_len // 2
+    sample_idx = np.arange(samples)[:, None]
+    slot_idx = np.arange(transform_len)[None, :]
+    freq_idx = np.where(slot_idx < half_len, slot_idx, slot_idx - half_len)
+    phases = sample_idx * freq_idx % transform_len
+    angles = phases.astype(np.float32) * np.float32(2.0 * math.pi / transform_len)
+    nyquist = np.where(sample_idx % 2 == 0, 1.0, -1.0)
+    basis = np.where(
+        slot_idx < half_len,
+        np.cos(angles),
+        np.where(slot_idx == half_len, nyquist, -np.sin(angles)),
+    )
+    return basis.astype(np.float32).astype(jnp.bfloat16)
+
+
+def inverse_table(transform_len, lag_total):
+    half_len = transform_len // 2
+    slot_idx = np.arange(transform_len)[:, None]
+    lag_idx = np.arange(lag_total)[None, :] - lag_total // 2
+    freq_idx = np.where(slot_idx < half_len, slot_idx, slot_idx - half_len)
+    phases = freq_idx * lag_idx % transform_len
+    angles = phases.astype(np.float32) * np.float32(2.0 * math.pi / transform_len)
+    weight = (np.where(freq_idx == 0, 1.0, 2.0) / transform_len).astype(np.float32)
+    nyquist = np.where(lag_idx % 2 == 0, 1.0, -1.0) / transform_len
+    basis = np.where(
+        slot_idx < half_len,
+        weight * np.cos(angles),
+        np.where(slot_idx == half_len, nyquist, -weight * np.sin(angles)),
+    )
+    return basis.astype(np.float32).astype(jnp.bfloat16)
 
 
 def each(count, step):
@@ -24,12 +58,33 @@
 
 
 def kernel(
-    rows, cols, x_ref, out_ref, stage, gathered, toeplitz, flat, waves, send_sem, recv_sem
+    rows,
+    cols,
+    x_ref,
+    forward_hbm,
+    inverse_hbm,
+    out_ref,
+    stage,
+    gathered,
+    forward,
+    inverse,
+    flat,
+    waves,
+    own,
+    cross,
+    send_sem,
+    recv_sem,
+    table_sem,
 ):
     n, comps, samples = x_ref.shape
     chunks = samples // LANES
-    span = samples + LANES
-    width = samples + 2 * LANES
+    half = forward.shape[1] // 2
+    tables = [
+        pltpu.make_async_copy(forward_hbm, forward, table_sem.at[0]),
+        pltpu.make_async_copy(inverse_hbm, inverse, table_sem.at[1]),
+    ]
+    for table in tables:
+        table.start()
     devices = rows * cols
     tall = rows // CORES
     wide = 2 ** int(math.log2(math.sqrt(cols)))
@@ -107,21 +162,6 @@
     each(plane - 1, lambda k: to_plane(mine, my_z, k).start())
     to_sibling(mine).start()
 
-    def build(t, c):
-        line = jnp.concatenate(
-            [normed[t][c : c + 1], jnp.zeros((1, LANES), jnp.float32)], axis=1
-        )
-        shifted = pltpu.roll(
-            jnp.broadcast_to(line, (LANES, span)), 0, axis=1, stride=1, stride_axis=0
-        )
-        toeplitz[t * LANES : (t + 1) * LANES, c * span : (c + 1) * span] = shifted.astype(
-            jnp.bfloat16
-        )
-
-    for t in range(1):
-        for c in range(comps):
-            build(t, c)
-
     def pass_on(k):
         z = up(k)
         slot = slot_of(my_xy, z, my_core)
@@ -131,15 +171,19 @@
 
     each(deep - 1, pass_on)
 
-    for t in range(1, n):
-        for c in range(comps):
-            build(t, c)
-    rows_block = waves.shape[0]
-    for c in range(comps):
-        for at in (0, LANES + samples):
-            waves[:, c * width + at : c * width + at + LANES] = jnp.zeros(
-                (rows_block, LANES), jnp.bfloat16
-            )
+    tables[0].wait()
+    bins = lax.broadcasted_iota(jnp.int32, (1, half), 1)
+    local = jnp.concatenate(normed, axis=0)
+    pad = -local.shape[0] % 16
+    local = jnp.concatenate([local, jnp.zeros((pad, samples), jnp.float32)], axis=0)
+    spectrum = jnp.dot(
+        local.astype(jnp.bfloat16), forward[...], preferred_element_type=jnp.float32
+    )
+    spectrum = spectrum.astype(jnp.bfloat16).astype(jnp.float32)
+    real, imag = spectrum[:, :half], spectrum[:, half:]
+    own[0] = real
+    own[1] = jnp.where(bins == 0, 0.0, imag)
+    own[2] = jnp.where(bins == 0, imag, real)
 
     def hand_over(k):
         slot = slot_of(beside(k // deep), (my_z + k % deep) % deep, my_core)
@@ -168,8 +212,10 @@
     lax.fori_loop(0, deep * (plane - 1), left_plane, 0)
     each(deep - 1, lambda k: to_column(k).wait_send())
 
+    rows_block = waves.shape[0] // comps
     block = rows_block // n
     stride = comps * chunks
+    tables[1].wait()
 
     def compare(b):
         flat[...] = (
@@ -179,32 +225,41 @@
         )
         for c in range(comps):
             for q in range(chunks):
-                at = c * width + (q + 1) * LANES
-                waves[:, at : at + LANES] = flat[
+                waves[c * rows_block : (c + 1) * rows_block, q * LANES : (q + 1) * LANES] = flat[
                     pl.ds(c * chunks + q, rows_block, stride=stride), :
                 ].astype(jnp.bfloat16)
 
-        best = None
-        for lag0 in range(-LAGS // 2, LAGS // 2, 2 * LANES):
-            low = max(0, -lag0 - LANES)
-            total = None
-            for c in range(comps):
-                left_part = toeplitz[:, c * span + low : c * span + low + samples]
-                at = c * width + LANES + low + lag0
-                right_part = jnp.concatenate(
-                    [waves[:, at : at + samples], waves[:, at + LANES : at + LANES + samples]],
-                    axis=0,
-                )
-                part = lax.dot_general(
-                    left_part,
-                    right_part,
-                    (((1,), (1,)), ((), ())),
-                    preferred_element_type=jnp.float32,
-                )
-                total = part if total is None else total + part
-            top = jnp.max(total.reshape(n, LANES, 2 * rows_block), axis=1)
-            best = top if best is None else jnp.maximum(best, top)
-        out_ref[b] = jnp.maximum(best[:, :rows_block], best[:, rows_block:])
+        for f in range(0, half, LANES):
+            g = half + f
+            basis = jnp.concatenate(
+                [forward[:, f : f + LANES], forward[:, g : g + LANES]], axis=1
+            )
+            spectra = jnp.dot(waves[...], basis, preferred_element_type=jnp.float32)
+            spectra = spectra.astype(jnp.bfloat16).astype(jnp.float32)
+            for j in range(0, rows_block, 16):
+                for i in range(n):
+                    even, odd = 0.0, 0.0
+                    for c in range(comps):
+                        at = c * rows_block + j
+                        real = spectra[at : at + 16, :LANES]
+                        imag = spectra[at : at + 16, LANES:]
+                        r = i * comps + c
+                        plain = own[0, r : r + 1, f : f + LANES]
+                        turned = own[1, r : r + 1, f : f + LANES]
+                        mixed = own[2, r : r + 1, f : f + LANES]
+                        even = even + (plain * real + turned * imag)
+                        odd = odd + (mixed * imag - turned * real)
+                    at = i * rows_block + j
+                    cross[at : at + 16, f : f + LANES] = even.astype(jnp.bfloat16)
+                    cross[at : at + 16, g : g + LANES] = odd.astype(jnp.bfloat16)
+
+        lagged = jnp.dot(cross[...], inverse[...], preferred_element_type=jnp.float32)
+        top = lagged[:, :LANES]
+        for at in range(LANES, LAGS, LANES):
+            top = jnp.maximum(top, lagged[:, at : at + LANES])
+        for i in range(n):
+            part = top[i * rows_block : (i + 1) * rows_block]
+            out_ref[b, i : i + 1] = jnp.max(part.T, axis=0, keepdims=True)
 
     each(devices // block, compare)
 
@@ -216,25 +271,30 @@
     devices = rows * cols
     block = math.gcd(devices, 32)
     chunks = samples // LANES
-    span = samples + LANES
-    width = samples + 2 * LANES
+    transform_len = samples + LAGS // 2
+    forward = forward_table(samples, transform_len)
+    inverse = inverse_table(transform_len, LAGS)
     vmem = pl.BlockSpec(memory_space=pltpu.VMEM)
     out = pl.pallas_call(
         functools.partial(kernel, rows, cols),
         out_shape=jax.ShapeDtypeStruct((devices // block, n, block * n), jnp.float32),
-        in_specs=[vmem],
+        in_specs=[vmem, pl.BlockSpec(memory_space=pl.ANY), pl.BlockSpec(memory_space=pl.ANY)],
         out_specs=vmem,
         scratch_shapes=[
             pltpu.VMEM((n * comps * chunks, LANES), jnp.float32),
             pltpu.VMEM((devices, n * comps, chunks, LANES), jnp.bfloat16),
-            pltpu.VMEM((n * LANES, comps * span), jnp.bfloat16),
+            pltpu.VMEM(forward.shape, jnp.bfloat16),
+            pltpu.VMEM(inverse.shape, jnp.bfloat16),
             pltpu.VMEM((block * n * comps * chunks, LANES), jnp.float32),
-            pltpu.VMEM((block * n, comps * width), jnp.bfloat16),
+            pltpu.VMEM((comps * block * n, samples), jnp.bfloat16),
+            pltpu.VMEM((3, n * comps + -(n * comps) % 16, transform_len // 2), jnp.float32),
+            pltpu.VMEM((n * block * n, transform_len), jnp.bfloat16),
             pltpu.SemaphoreType.DMA((2 * devices + cols,)),
             pltpu.SemaphoreType.DMA((devices,)),
+            pltpu.SemaphoreType.DMA((2,)),
         ],
         compiler_params=pltpu.CompilerParams(collective_id=0, has_side_effects=True),
-    )(templates)
+    )(templates, forward, inverse)
     return out.transpose(1, 0, 2).reshape(n, devices * n)
 
 

time: 19 us -> 19.5 us (1.026)
  Pallas kernels: 17.4 us -> 17.9 us
    pallas_call x1, Pallas kernels: 17.4 us -> 17.9 us  [body(): pl.pallas_call(functools.partial(kernel, rows, cols), out_shape=jax.Shape...]
where the time goes in v2:
time: 19.5 us; the launch traced here: 19.2 us
  Pallas kernels  17.9 us (92%)
  local copies, waits for them, and re-layouts  1.26 us (6%)
    pallas_call x1, Pallas kernels, body(): pl.pallas_call(functools.partial(kernel, rows, cols), out_shape=jax.Shape...  17.9 us
    unnamed x1, local copies, waits for them, and re-layouts  1.26 us

profile of v2, /device:TPU:0, one launch (start us, length us, event | category | flops | bytes accessed | tf_op | source)
XLA Modules:
  0.0 19.2 jit_solution(17765305758111092052)
XLA Ops:
  0.0 17.9 %shard_map.37 = f32[1,3,96]{2,1,0:T(4,128)} custom-call(f32[3,3,1024]{2,1,0:T(4,128)} %x_ref.1, bf16[1024,1280]{1,0:T(8,128)(2,1)} %constant.4.clone.forward_hbm, bf16[1280,512]{1,0:T(8,128)(2,1)} %constant.5.clone.inverse_hbm), custom_call_target="tpu_custom_call" | custom-call | tf_op jit(solution)/shard_map/pallas_call | solution.py:278
  17.9 1.3 %copy.5 = f32[3,96]{1,0:T(4,128)} copy(f32[3,96]{1,0:T(4,128)} %bitcast.1) | data formatting | bytes 2304

commit v3 on v2

--- a/solution.py
+++ b/solution.py
@@ -72,12 +72,16 @@
     waves,
     own,
     cross,
+    outgoing,
+    incoming,
     send_sem,
     recv_sem,
     table_sem,
+    result_sem,
 ):
     n, comps, samples = x_ref.shape
     chunks = samples // LANES
+    lines = n * comps * chunks
     half = forward.shape[1] // 2
     tables = [
         pltpu.make_async_copy(forward_hbm, forward, table_sem.at[0]),
@@ -85,11 +89,11 @@
     ]
     for table in tables:
         table.start()
-    devices = rows * cols
     tall = rows // CORES
     wide = 2 ** int(math.log2(math.sqrt(cols)))
     deep = cols // wide
     plane = tall * wide
+    slots = plane * deep
     row = lax.axis_index("row")
     col = lax.axis_index("col")
     my_y, my_core = row // CORES, row % CORES
@@ -99,18 +103,22 @@
     def place(xy, z, core):
         return (xy // wide) * CORES + core, z * wide + xy % wide
 
-    def slot_of(xy, z, core):
-        r, c = place(xy, z, core)
-        return r * cols + c
+    def slot_of(xy, z):
+        return (xy // wide) * cols + z * wide + xy % wide
 
     def up(k):
-        return (my_z + 1 + k) % deep
+        if deep & (deep - 1):
+            return (my_z + 1 + k) % deep
+        z, bit = 0, 1
+        while bit < deep:
+            z, bit = z + (my_z // bit + (1 + k) // bit) % 2 * bit, bit * 2
+        return z
 
     def beside(k):
         return (my_xy + 1 + k) % plane
 
     other = 1 - my_core
-    mine = slot_of(my_xy, my_z, my_core)
+    mine = slot_of(my_xy, my_z)
 
     barrier = pltpu.get_barrier_semaphore()
 
@@ -123,99 +131,89 @@
     each(plane - 1, lambda k: greet(beside(k), my_z, my_core))
     greet(my_xy, my_z, other)
 
-    normed = []
     for t in range(n):
         x = x_ref[t]
         scale = lax.rsqrt(jnp.mean(x * x, axis=1, keepdims=True) + 1e-06) / math.sqrt(samples)
         rounded = (x * scale).astype(jnp.bfloat16).astype(jnp.float32)
-        normed.append(rounded)
         for q in range(chunks):
             stage[pl.ds(t * comps * chunks + q, comps, stride=chunks), :] = rounded[
                 :, q * LANES : (q + 1) * LANES
             ]
-    gathered[mine] = stage[...].reshape(n * comps, chunks, LANES).astype(jnp.bfloat16)
+    gathered[mine] = stage[:lines].reshape(n * comps, chunks, LANES).astype(jnp.bfloat16)
     pl.semaphore_wait(barrier, deep - 1 + plane - 1 + 1)
 
-    def copy(slot, to, sem):
+    def copy(slot, to, sem, landing=None):
+        landing = slot if landing is None else landing
         return pltpu.make_async_remote_copy(
             src_ref=gathered.at[slot],
-            dst_ref=gathered.at[slot],
+            dst_ref=gathered.at[landing],
             send_sem=send_sem.at[sem],
-            recv_sem=recv_sem.at[slot],
+            recv_sem=recv_sem.at[landing],
             device_id=to,
             device_id_type=MESH,
         )
 
-    def to_sibling(slot):
-        return copy(slot, place(my_xy, my_z, other), slot)
-
     def to_plane(slot, z, k):
-        return copy(slot, place(beside(k), my_z, my_core), devices + z * plane + k)
+        return copy(slot, place(beside(k), my_z, my_core), z * plane + k)
 
     def to_column(k):
-        return copy(mine, place(my_xy, up(k), my_core), devices + deep * plane + k)
+        return copy(mine, place(my_xy, up(k), my_core), slots + k)
+
+    def to_sibling():
+        return copy(mine, place(my_xy, my_z, other), slots + deep, slots)
 
     def arrived(slot):
-        to_sibling(slot).wait_recv()
-
-    each(deep - 1, lambda k: to_column(k).start())
+        copy(slot, place(my_xy, my_z, other), slots + deep).wait_recv()
+
+    each(deep - 1, lambda k: to_column(deep - 2 - k).start())
+    to_sibling().start()
     each(plane - 1, lambda k: to_plane(mine, my_z, k).start())
-    to_sibling(mine).start()
-
-    def pass_on(k):
-        z = up(k)
-        slot = slot_of(my_xy, z, my_core)
-        arrived(slot)
-        each(plane - 1, lambda m: to_plane(slot, z, m).start())
-        to_sibling(slot).start()
-
-    each(deep - 1, pass_on)
-
+
+    arrived(slots)
+    stage[lines:] = gathered[slots].astype(jnp.float32).reshape(lines, LANES)
     tables[0].wait()
-    bins = lax.broadcasted_iota(jnp.int32, (1, half), 1)
-    local = jnp.concatenate(normed, axis=0)
-    pad = -local.shape[0] % 16
+    local = jnp.concatenate(
+        [stage[pl.ds(q, CORES * n * comps, stride=chunks), :] for q in range(chunks)], axis=1
+    )
+    pad = own.shape[1] - local.shape[0]
     local = jnp.concatenate([local, jnp.zeros((pad, samples), jnp.float32)], axis=0)
     spectrum = jnp.dot(
         local.astype(jnp.bfloat16), forward[...], preferred_element_type=jnp.float32
     )
     spectrum = spectrum.astype(jnp.bfloat16).astype(jnp.float32)
     real, imag = spectrum[:, :half], spectrum[:, half:]
+    bins = lax.broadcasted_iota(jnp.int32, (1, half), 1)
     own[0] = real
     own[1] = jnp.where(bins == 0, 0.0, imag)
     own[2] = jnp.where(bins == 0, imag, real)
 
-    def hand_over(k):
-        slot = slot_of(beside(k // deep), (my_z + k % deep) % deep, my_core)
+    def pass_on(k):
+        z = up(k)
+        slot = slot_of(my_xy, z)
         arrived(slot)
-        to_sibling(slot).start()
-
-    each_loop = (plane - 1) * deep
-    lax.fori_loop(0, each_loop, lambda k, carry: (hand_over(k), carry)[1], 0)
-
-    def from_sibling(k, carry):
-        arrived(slot_of(k // deep, k % deep, other))
-        return carry
-
-    lax.fori_loop(0, plane * deep, from_sibling, 0)
-
-    def left(k, carry):
-        to_sibling(slot_of(k // deep, k % deep, my_core)).wait_send()
-        return carry
-
-    lax.fori_loop(0, plane * deep, left, 0)
-
-    def left_plane(k, carry):
-        to_plane(mine, k // (plane - 1), k % (plane - 1)).wait_send()
-        return carry
-
-    lax.fori_loop(0, deep * (plane - 1), left_plane, 0)
-    each(deep - 1, lambda k: to_column(k).wait_send())
+        each(plane - 1, lambda m: to_plane(slot, z, m).start())
+
+    each(deep - 1, pass_on)
+    tables[1].wait()
+    each(
+        (plane - 1) * deep,
+        lambda k: arrived(slot_of(beside(k // deep), (my_z + k % deep) % deep)),
+    )
 
     rows_block = waves.shape[0] // comps
     block = rows_block // n
+    blocks = slots // block
     stride = comps * chunks
-    tables[1].wait()
+
+    def result(b):
+        return pltpu.make_async_remote_copy(
+            src_ref=outgoing.at[b],
+            dst_ref=incoming.at[b],
+            send_sem=result_sem.at[b],
+            recv_sem=result_sem.at[blocks + b],
+            device_id=place(my_xy, my_z, other),
+            device_id_type=MESH,
+        )
 
     def compare(b):
         flat[...] = (
@@ -237,7 +235,7 @@
             spectra = jnp.dot(waves[...], basis, preferred_element_type=jnp.float32)
             spectra = spectra.astype(jnp.bfloat16).astype(jnp.float32)
             for j in range(0, rows_block, 16):
-                for i in range(n):
+                for i in range(CORES * n):
                     even, odd = 0.0, 0.0
                     for c in range(comps):
                         at = c * rows_block + j
@@ -253,49 +251,95 @@
                     cross[at : at + 16, f : f + LANES] = even.astype(jnp.bfloat16)
                     cross[at : at + 16, g : g + LANES] = odd.astype(jnp.bfloat16)
 
-        lagged = jnp.dot(cross[...], inverse[...], preferred_element_type=jnp.float32)
-        top = lagged[:, :LANES]
-        for at in range(LANES, LAGS, LANES):
-            top = jnp.maximum(top, lagged[:, at : at + LANES])
-        for i in range(n):
-            part = top[i * rows_block : (i + 1) * rows_block]
-            out_ref[b, i : i + 1] = jnp.max(part.T, axis=0, keepdims=True)
-
-    each(devices // block, compare)
+        def similar(core):
+            first = core * n * rows_block
+            lagged = jnp.dot(
+                cross[first : first + n * rows_block],
+                inverse[...],
+                preferred_element_type=jnp.float32,
+            )
+            top = lagged[:, :LANES]
+            for at in range(LANES, LAGS, LANES):
+                top = jnp.maximum(top, lagged[:, at : at + LANES])
+            flipped = jnp.max(top.T, axis=0, keepdims=True)
+            return jnp.concatenate(
+                [flipped[:, i * rows_block : (i + 1) * rows_block] for i in range(n)], axis=0
+            )
+
+        outgoing[b] = similar(1)
+        result(b).start()
+        out = similar(0)
+        result(b).wait_recv()
+        theirs = incoming[b]
+        low = jnp.where(my_core == 0, out, theirs)
+        high = jnp.where(my_core == 0, theirs, out)
+        if blocks == 1:
+            part = cols * n
+            out_ref[...] = jnp.concatenate(
+                [
+                    kind[:, y * part : (y + 1) * part]
+                    for y in range(tall)
+                    for kind in (low, high)
+                ],
+                axis=1,
+            )
+        else:
+            out_ref[b, 0] = low
+            out_ref[b, 1] = high
+        result(b).wait_send()
+
+    each(blocks, compare)
+
+    each(
+        deep * (plane - 1),
+        lambda k: to_plane(mine, k // (plane - 1), k % (plane - 1)).wait_send(),
+    )
+    each(deep - 1, lambda k: to_column(k).wait_send())
+    to_sibling().wait_send()
 
 
 def body(templates):
     n, comps, samples = templates.shape
     rows = lax.axis_size("row")
     cols = lax.axis_size("col")
-    devices = rows * cols
-    block = math.gcd(devices, 32)
+    slots = rows * cols // CORES
+    block = math.gcd(slots, 16)
+    blocks = slots // block
     chunks = samples // LANES
     transform_len = samples + LAGS // 2
     forward = forward_table(samples, transform_len)
     inverse = inverse_table(transform_len, LAGS)
     vmem = pl.BlockSpec(memory_space=pltpu.VMEM)
+    hbm = pl.BlockSpec(memory_space=pl.ANY)
+    local = CORES * n * comps
+    shape = (n, CORES * slots * n) if blocks == 1 else (blocks, CORES, n, block * n)
     out = pl.pallas_call(
         functools.partial(kernel, rows, cols),
-        out_shape=jax.ShapeDtypeStruct((devices // block, n, block * n), jnp.float32),
-        in_specs=[vmem, pl.BlockSpec(memory_space=pl.ANY), pl.BlockSpec(memory_space=pl.ANY)],
+        out_shape=jax.ShapeDtypeStruct(shape, jnp.float32),
+        in_specs=[vmem, hbm, hbm],
         out_specs=vmem,
         scratch_shapes=[
-            pltpu.VMEM((n * comps * chunks, LANES), jnp.float32),
-            pltpu.VMEM((devices, n * comps, chunks, LANES), jnp.bfloat16),
+            pltpu.VMEM((CORES * n * comps * chunks, LANES), jnp.float32),
+            pltpu.VMEM((slots + 1, n * comps, chunks, LANES), jnp.bfloat16),
             pltpu.VMEM(forward.shape, jnp.bfloat16),
             pltpu.VMEM(inverse.shape, jnp.bfloat16),
             pltpu.VMEM((block * n * comps * chunks, LANES), jnp.float32),
             pltpu.VMEM((comps * block * n, samples), jnp.bfloat16),
-            pltpu.VMEM((3, n * comps + -(n * comps) % 16, transform_len // 2), jnp.float32),
-            pltpu.VMEM((n * block * n, transform_len), jnp.bfloat16),
-            pltpu.SemaphoreType.DMA((2 * devices + cols,)),
-            pltpu.SemaphoreType.DMA((devices,)),
+            pltpu.VMEM((3, local + -local % 16, transform_len // 2), jnp.float32),
+            pltpu.VMEM((CORES * n * block * n, transform_len), jnp.bfloat16),
+            pltpu.VMEM((blocks, n, block * n), jnp.float32),
+            pltpu.VMEM((blocks, n, block * n), jnp.float32),
+            pltpu.SemaphoreType.DMA((slots + cols + 1,)),
+            pltpu.SemaphoreType.DMA((slots + 1,)),
             pltpu.SemaphoreType.DMA((2,)),
+            pltpu.SemaphoreType.DMA((2 * blocks,)),
         ],
         compiler_params=pltpu.CompilerParams(collective_id=0, has_side_effects=True),
     )(templates, forward, inverse)
-    return out.transpose(1, 0, 2).reshape(n, devices * n)
+    if blocks == 1:
+        return out
+    out = out.transpose(2, 1, 0, 3).reshape(n, CORES, rows // CORES, cols * n)
+    return out.transpose(0, 2, 1, 3).reshape(n, CORES * slots * n)
 
 
 def solution(mesh):

time: 19.5 us -> 18.2 us (0.933)
  Pallas kernels: 17.9 us -> 16.8 us
    pallas_call x1, Pallas kernels: 17.9 us -> 16.8 us  [body(): pl.pallas_call(functools.partial(kernel, rows, cols), out_shape=jax.Shape...]
where the time goes in v3:
time: 18.2 us; the launch traced here: 18 us
  Pallas kernels  16.8 us (92%)
  local copies, waits for them, and re-layouts  1.26 us (7%)
    pallas_call x1, Pallas kernels, body(): pl.pallas_call(functools.partial(kernel, rows, cols), out_shape=jax.Shape...  16.8 us
    unnamed x1, local copies, waits for them, and re-layouts  1.26 us

profile of v3, /device:TPU:0, one launch (start us, length us, event | category | flops | bytes accessed | tf_op | source)
XLA Modules:
  0.0 18.0 jit_solution(17429170270668984600)
XLA Ops:
  0.0 16.8 %shard_map.37 = f32[3,96]{1,0:T(4,128)} custom-call(f32[3,3,1024]{2,1,0:T(4,128)} %x_ref.1, bf16[1024,1280]{1,0:T(8,128)(2,1)} %constant.4.clone.forward_hbm, bf16[1280,512]{1,0:T(8,128)(2,1)} %constant.5.clone.inverse_hbm), custom_call_target="tpu_custom_call" | custom-call | tf_op jit(solution)/shard_map/pallas_call | solution.py:316
  16.8 1.3 %copy.5 = f32[3,96]{1,0:T(4,128)} copy(f32[3,96]{1,0:T(4,128)} %shard_map.37) | data formatting | bytes 2304

commit v4 on v3

--- a/solution.py
+++ b/solution.py
@@ -60,10 +60,11 @@
 def kernel(
     rows,
     cols,
-    x_ref,
+    x_hbm,
     forward_hbm,
     inverse_hbm,
     out_ref,
+    x_ref,
     stage,
     gathered,
     forward,
@@ -71,6 +72,7 @@
     flat,
     waves,
     own,
+    spectra,
     cross,
     outgoing,
     incoming,
@@ -87,8 +89,6 @@
         pltpu.make_async_copy(forward_hbm, forward, table_sem.at[0]),
         pltpu.make_async_copy(inverse_hbm, inverse, table_sem.at[1]),
     ]
-    for table in tables:
-        table.start()
     tall = rows // CORES
     wide = 2 ** int(math.log2(math.sqrt(cols)))
     deep = cols // wide
@@ -130,6 +130,12 @@
     each(deep - 1, lambda k: greet(my_xy, up(k), my_core))
     each(plane - 1, lambda k: greet(beside(k), my_z, my_core))
     greet(my_xy, my_z, other)
+
+    taken = pltpu.make_async_copy(x_hbm, x_ref, table_sem.at[2])
+    taken.start()
+    for table in tables:
+        table.start()
+    taken.wait()
 
     for t in range(n):
         x = x_ref[t]
@@ -232,26 +238,33 @@
             basis = jnp.concatenate(
                 [forward[:, f : f + LANES], forward[:, g : g + LANES]], axis=1
             )
-            spectra = jnp.dot(waves[...], basis, preferred_element_type=jnp.float32)
-            spectra = spectra.astype(jnp.bfloat16).astype(jnp.float32)
-            for j in range(0, rows_block, 16):
-                for i in range(CORES * n):
-                    even, odd = 0.0, 0.0
-                    for c in range(comps):
-                        at = c * rows_block + j
-                        real = spectra[at : at + 16, :LANES]
-                        imag = spectra[at : at + 16, LANES:]
-                        r = i * comps + c
-                        plain = own[0, r : r + 1, f : f + LANES]
-                        turned = own[1, r : r + 1, f : f + LANES]
-                        mixed = own[2, r : r + 1, f : f + LANES]
-                        even = even + (plain * real + turned * imag)
-                        odd = odd + (mixed * imag - turned * real)
-                    at = i * rows_block + j
-                    cross[at : at + 16, f : f + LANES] = even.astype(jnp.bfloat16)
-                    cross[at : at + 16, g : g + LANES] = odd.astype(jnp.bfloat16)
+            found = jnp.dot(waves[...], basis, preferred_element_type=jnp.float32)
+            found = found.astype(jnp.bfloat16).astype(jnp.float32)
+            spectra[:, f : f + LANES] = found[:, :LANES]
+            spectra[:, g : g + LANES] = found[:, LANES:]
+
+        def multiply(core):
+            for f in range(0, half, LANES):
+                g = half + f
+                for j in range(0, rows_block, 16):
+                    for i in range(core * n, (core + 1) * n):
+                        even, odd = 0.0, 0.0
+                        for c in range(comps):
+                            at = c * rows_block + j
+                            real = spectra[at : at + 16, f : f + LANES]
+                            imag = spectra[at : at + 16, g : g + LANES]
+                            r = i * comps + c
+                            plain = own[0, r : r + 1, f : f + LANES]
+                            turned = own[1, r : r + 1, f : f + LANES]
+                            mixed = own[2, r : r + 1, f : f + LANES]
+                            even = even + (plain * real + turned * imag)
+                            odd = odd + (mixed * imag - turned * real)
+                        at = i * rows_block + j
+                        cross[at : at + 16, f : f + LANES] = even.astype(jnp.bfloat16)
+                        cross[at : at + 16, g : g + LANES] = odd.astype(jnp.bfloat16)
 
         def similar(core):
+            multiply(core)
             first = core * n * rows_block
             lagged = jnp.dot(
                 cross[first : first + n * rows_block],
@@ -310,15 +323,16 @@
     forward = forward_table(samples, transform_len)
     inverse = inverse_table(transform_len, LAGS)
     vmem = pl.BlockSpec(memory_space=pltpu.VMEM)
-    hbm = pl.BlockSpec(memory_space=pl.ANY)
+    hbm = pl.BlockSpec(memory_space=pltpu.HBM)
     local = CORES * n * comps
     shape = (n, CORES * slots * n) if blocks == 1 else (blocks, CORES, n, block * n)
     out = pl.pallas_call(
         functools.partial(kernel, rows, cols),
-        out_shape=jax.ShapeDtypeStruct(shape, jnp.float32),
-        in_specs=[vmem, hbm, hbm],
+        out_shape=pltpu.VMEM(shape, jnp.float32),
+        in_specs=[hbm, hbm, hbm],
         out_specs=vmem,
         scratch_shapes=[
+            pltpu.VMEM(templates.shape, jnp.float32),
             pltpu.VMEM((CORES * n * comps * chunks, LANES), jnp.float32),
             pltpu.VMEM((slots + 1, n * comps, chunks, LANES), jnp.bfloat16),
             pltpu.VMEM(forward.shape, jnp.bfloat16),
@@ -326,12 +340,13 @@
             pltpu.VMEM((block * n * comps * chunks, LANES), jnp.float32),
             pltpu.VMEM((comps * block * n, samples), jnp.bfloat16),
             pltpu.VMEM((3, local + -local % 16, transform_len // 2), jnp.float32),
+            pltpu.VMEM((comps * block * n, transform_len), jnp.float32),
             pltpu.VMEM((CORES * n * block * n, transform_len), jnp.bfloat16),
             pltpu.VMEM((blocks, n, block * n), jnp.float32),
             pltpu.VMEM((blocks, n, block * n), jnp.float32),
             pltpu.SemaphoreType.DMA((slots + cols + 1,)),
             pltpu.SemaphoreType.DMA((slots + 1,)),
-            pltpu.SemaphoreType.DMA((2,)),
+            pltpu.SemaphoreType.DMA((3,)),
             pltpu.SemaphoreType.DMA((2 * blocks,)),
         ],
         compiler_params=pltpu.CompilerParams(collective_id=0, has_side_effects=True),

time: 18.2 us -> 15.7 us (0.86)
  Pallas kernels: 16.8 us -> 14.9 us
  local copies, waits for them, and re-layouts: 1.26 us -> 0.58 us
    pallas_call x1, Pallas kernels: 16.8 us -> 14.9 us  [body(): pl.pallas_call(functools.partial(kernel, rows, cols), out_shape=pltpu.VME...]
    unnamed x1, local copies, waits for them, and re-layouts: 1.26 us -> 0.58 us
where the time goes in v4:
time: 15.7 us; the launch traced here: 15.5 us
  Pallas kernels  14.9 us (95%)
  local copies, waits for them, and re-layouts  0.58 us (4%)
    pallas_call x1, Pallas kernels, body(): pl.pallas_call(functools.partial(kernel, rows, cols), out_shape=pltpu.VME...  14.9 us
    unnamed x1, local copies, waits for them, and re-layouts  0.58 us

profile of v4, /device:TPU:0, one launch (start us, length us, event | category | flops | bytes accessed | tf_op | source)
XLA Modules:
  0.0 15.5 jit_solution(6221527026292616387)
XLA Ops:
  0.0 14.9 %shard_map.37 = f32[3,96]{1,0:T(4,128)S(1)} custom-call(f32[3,3,1024]{2,1,0:T(4,128)} %x_hbm.1, bf16[1024,1280]{1,0:T(8,128)(2,1)} %constant.4.clone.forward_hbm, bf16[1280,512]{1,0:T(8,128)(2,1)} %constant.5.clone.inverse_hbm), custom_call_target="tpu_custom_call" | custom-call | tf_op jit(solution)/shard_map/pallas_call | solution.py:329
  14.9 0.6 %copy.5 = f32[3,96]{1,0:T(4,128)} copy(f32[3,96]{1,0:T(4,128)S(1)} %shard_map.37) | data formatting | bytes 2304

commit v5 on v4

--- a/solution.py
+++ b/solution.py
@@ -106,16 +106,19 @@
     def slot_of(xy, z):
         return (xy // wide) * cols + z * wide + xy % wide
 
+    def partner(me, count, k):
+        if count & (count - 1):
+            return (me + k) % count
+        found, bit = 0, 1
+        while bit < count:
+            found, bit = found + (me // bit + k // bit) % 2 * bit, bit * 2
+        return found
+
     def up(k):
-        if deep & (deep - 1):
-            return (my_z + 1 + k) % deep
-        z, bit = 0, 1
-        while bit < deep:
-            z, bit = z + (my_z // bit + (1 + k) // bit) % 2 * bit, bit * 2
-        return z
+        return partner(my_z, deep, 1 + k)
 
     def beside(k):
-        return (my_xy + 1 + k) % plane
+        return partner(my_xy, plane, plane - 1 - k)
 
     other = 1 - my_core
     mine = slot_of(my_xy, my_z)
@@ -175,6 +178,21 @@
     to_sibling().start()
     each(plane - 1, lambda k: to_plane(mine, my_z, k).start())
 
+    rows_block = waves.shape[0] // comps
+    block = rows_block // n
+    blocks = slots // block
+
+    def unpack(slot):
+        at = pl.multiple_of(slot * lines, SUBS)
+        flat[pl.ds(at, lines), :] = gathered[slot].astype(jnp.float32).reshape(lines, LANES)
+
+    def pass_on(k):
+        z = up(k)
+        slot = slot_of(my_xy, z)
+        arrived(slot)
+        each(plane - 1, lambda m: to_plane(slot, z, m).start())
+
+    each(deep - 1, pass_on)
     arrived(slots)
     stage[lines:] = gathered[slots].astype(jnp.float32).reshape(lines, LANES)
     tables[0].wait()
@@ -193,22 +211,19 @@
     own[1] = jnp.where(bins == 0, 0.0, imag)
     own[2] = jnp.where(bins == 0, imag, real)
 
-    def pass_on(k):
-        z = up(k)
-        slot = slot_of(my_xy, z)
+    tables[1].wait()
+    if blocks == 1:
+        for k in range(deep):
+            unpack(slot_of(my_xy, k))
+
+    def take(k):
+        slot = slot_of(beside(k % (plane - 1)), partner(my_z, deep, k // (plane - 1)))
         arrived(slot)
-        each(plane - 1, lambda m: to_plane(slot, z, m).start())
-
-    each(deep - 1, pass_on)
-    tables[1].wait()
-    each(
-        (plane - 1) * deep,
-        lambda k: arrived(slot_of(beside(k // deep), (my_z + k % deep) % deep)),
-    )
-
-    rows_block = waves.shape[0] // comps
-    block = rows_block // n
-    blocks = slots // block
+        if blocks == 1:
+            unpack(slot)
+
+    lax.fori_loop(0, (plane - 1) * deep, lambda k, carry: (take(k), carry)[1], 0)
+
     stride = comps * chunks
 
     def result(b):
@@ -222,17 +237,37 @@
         )
 
     def compare(b):
-        flat[...] = (
-            gathered[pl.ds(b * block, block)]
-            .astype(jnp.float32)
-            .reshape(block * n * comps * chunks, LANES)
-        )
+        if blocks > 1:
+            flat[...] = (
+                gathered[pl.ds(b * block, block)]
+                .astype(jnp.float32)
+                .reshape(block * n * comps * chunks, LANES)
+            )
         for c in range(comps):
             for q in range(chunks):
                 waves[c * rows_block : (c + 1) * rows_block, q * LANES : (q + 1) * LANES] = flat[
                     pl.ds(c * chunks + q, rows_block, stride=stride), :
                 ].astype(jnp.bfloat16)
 
+        def multiply(core, f):
+            g = half + f
+            for j in range(0, rows_block, 16):
+                for i in range(core * n, (core + 1) * n):
+                    even, odd = 0.0, 0.0
+                    for c in range(comps):
+                        at = c * rows_block + j
+                        real = spectra[at : at + 16, f : f + LANES]
+                        imag = spectra[at : at + 16, g : g + LANES]
+                        r = i * comps + c
+                        plain = own[0, r : r + 1, f : f + LANES]
+                        turned = own[1, r : r + 1, f : f + LANES]
+                        mixed = own[2, r : r + 1, f : f + LANES]
+                        even = even + (plain * real + turned * imag)
+                        odd = odd + (mixed * imag - turned * real)
+                    at = i * rows_block + j
+                    cross[at : at + 16, f : f + LANES] = even.astype(jnp.bfloat16)
+                    cross[at : at + 16, g : g + LANES] = odd.astype(jnp.bfloat16)
+
         for f in range(0, half, LANES):
             g = half + f
             basis = jnp.concatenate(
@@ -242,29 +277,12 @@
             found = found.astype(jnp.bfloat16).astype(jnp.float32)
             spectra[:, f : f + LANES] = found[:, :LANES]
             spectra[:, g : g + LANES] = found[:, LANES:]
-
-        def multiply(core):
-            for f in range(0, half, LANES):
-                g = half + f
-                for j in range(0, rows_block, 16):
-                    for i in range(core * n, (core + 1) * n):
-                        even, odd = 0.0, 0.0
-                        for c in range(comps):
-                            at = c * rows_block + j
-                            real = spectra[at : at + 16, f : f + LANES]
-                            imag = spectra[at : at + 16, g : g + LANES]
-                            r = i * comps + c
-                            plain = own[0, r : r + 1, f : f + LANES]
-                            turned = own[1, r : r + 1, f : f + LANES]
-                            mixed = own[2, r : r + 1, f : f + LANES]
-                            even = even + (plain * real + turned * imag)
-                            odd = odd + (mixed * imag - turned * real)
-                        at = i * rows_block + j
-                        cross[at : at + 16, f : f + LANES] = even.astype(jnp.bfloat16)
-                        cross[at : at + 16, g : g + LANES] = odd.astype(jnp.bfloat16)
+            multiply(1, f)
 
         def similar(core):
-            multiply(core)
+            if core == 0:
+                for f in range(0, half, LANES):
+                    multiply(0, f)
             first = core * n * rows_block
             lagged = jnp.dot(
                 cross[first : first + n * rows_block],

time: 15.7 us -> 15.7 us (level)
  no operation moved by 1% of the time
where the time goes in v5:
time: 15.7 us; the launch traced here: 15.5 us
  Pallas kernels  14.9 us (95%)
  local copies, waits for them, and re-layouts  0.58 us (4%)
    pallas_call x1, Pallas kernels, body(): pl.pallas_call(functools.partial(kernel, rows, cols), out_shape=pltpu.VME...  14.9 us
    unnamed x1, local copies, waits for them, and re-layouts  0.58 us

profile of v5, /device:TPU:0, one launch (start us, length us, event | category | flops | bytes accessed | tf_op | source)
XLA Modules:
  0.0 15.5 jit_solution(11105658114739023538)
XLA Ops:
  0.0 14.9 %shard_map.37 = f32[3,96]{1,0:T(4,128)S(1)} custom-call(f32[3,3,1024]{2,1,0:T(4,128)} %x_hbm.1, bf16[1024,1280]{1,0:T(8,128)(2,1)} %constant.4.clone.forward_hbm, bf16[1280,512]{1,0:T(8,128)(2,1)} %constant.5.clone.inverse_hbm), custom_call_target="tpu_custom_call" | custom-call | tf_op jit(solution)/shard_map/pallas_call | solution.py:347
  14.9 0.6 %copy.5 = f32[3,96]{1,0:T(4,128)} copy(f32[3,96]{1,0:T(4,128)S(1)} %shard_map.37) | data formatting | bytes 2304
